TPU v7x, 32 devices: a whole 2x2x4 slice. The times are simulated.
32 devices in a mesh: grp: 4 (over y, core), blk: 8 (over z, x).
Axes of the slice: x: 2, y: 2, z: 4, core: 2. Of those that a mesh axis runs over, the one named last changes fastest.
Arguments:
- queries: bfloat16 [4, 128, 4096], P(None, ('blk', 'grp')), may hold values from -24 to 24
- cache_keys: bfloat16 [4, 3584, 512], P('grp', 'blk'), may hold values from -24 to 24
- cache_values: bfloat16 [4, 3584, 512], P('grp', 'blk'), may hold values from -15 to 15
- new_keys: bfloat16 [4, 128, 512], P(None, ('blk', 'grp')), may hold values from -6 to 6
- new_values: bfloat16 [4, 128, 512], P(None, ('blk', 'grp')), may hold values from -15 to 15
- hits: int32 [4], P('grp'), may hold values from 448 to 3584, as said below
- counts: int32 [4], P('grp'), may hold values from 64 to 128, as said below
- assign: int32 [4, 8], P('grp'), may hold values from 0 to 7, each once within a row
Outputs:
- attended: bfloat16 [4, 128, 4096], P(None, ('blk', 'grp'))
Inputs may be any that keep to these rules, and one draw needn't show every extreme that they name: Cached positions of request r below hits[r] are valid; in every draw some request has all 3584 valid. New tokens of request r at order counts[r] or later are padding; in every draw some request has all 128.
All inputs are finite; a program needn't handle non-finite values.
Results may differ from a plain program's by a relative error of at most 0.0085.
Values may be sent and summed in bfloat16 or wider, within the bound.
A program may use at most 128 MiB of HBM per device.

v0:
```python
import jax
import jax.numpy as jnp
from jax import lax
from jax.sharding import PartitionSpec as P

HEAD_DIM = 128


def shifted(value, axis, by):
    length = lax.axis_size(axis)
    return lax.ppermute(value, axis, [(i, (i + by) % length) for i in range(length)])


def partial_block(queries, keys, values, allowed, kv_heads):
    row_count, full_width = queries.shape
    key_count = keys.shape[0]
    head_dim = keys.shape[1] // kv_heads
    group_size = full_width // head_dim // kv_heads
    query_heads = queries.reshape(row_count, kv_heads, group_size, head_dim)
    key_heads = keys.reshape(key_count, kv_heads, head_dim)
    scores = jnp.einsum(
        "qkgd,nkd->kgqn", query_heads, key_heads, preferred_element_type=jnp.float32
    ) * head_dim ** (-0.5)
    scores = jnp.where(allowed[None, None], scores, -1e30)
    block_max = jnp.max(scores, axis=-1)
    exp_terms = jnp.where(allowed[None, None], jnp.exp(scores - block_max[..., None]), 0.0)
    weight_sum = jnp.sum(exp_terms, axis=-1)
    prob_bf = exp_terms.astype(jnp.bfloat16)
    value_heads = values.reshape(key_count, kv_heads, head_dim)
    blended = jnp.einsum("kgqn,nkd->qkgd", prob_bf, value_heads, preferred_element_type=jnp.float32)
    floor_sum = jnp.maximum(weight_sum, 1.0).transpose(2, 0, 1)[..., None]
    blended = (blended / floor_sum).reshape(row_count, full_width).astype(jnp.bfloat16)
    maxima = block_max.transpose(2, 0, 1).reshape(row_count, -1)
    weights = weight_sum.transpose(2, 0, 1).reshape(row_count, -1)
    return (blended, maxima, weights)


def combine(running, part, head_count):
    summed, maxima, weights = running
    blended, part_max, part_weight = part
    row_count, full_width = summed.shape
    highest = jnp.maximum(maxima, part_max)
    old_scale = jnp.exp(maxima - highest)
    new_scale = part_weight * jnp.exp(part_max - highest)
    summed = summed.reshape(row_count, head_count, -1) * old_scale[:, :, None]
    summed = summed + new_scale[:, :, None] * blended.astype(jnp.float32).reshape(
        row_count, head_count, -1
    )
    return (summed.reshape(row_count, full_width), highest, weights * old_scale + new_scale)


def local(queries, cache_keys, cache_values, new_keys, new_values, hits, counts, assign):
    local_q, local_k, local_v = (
        lax.all_to_all(queries, "grp", split_axis=0, concat_axis=1, tiled=True),
        lax.all_to_all(new_keys, "grp", split_axis=0, concat_axis=1, tiled=True),
        lax.all_to_all(new_values, "grp", split_axis=0, concat_axis=1, tiled=True),
    )
    local_q = local_q[0]
    local_k = local_k[0]
    local_v = local_v[0]
    row_count, full_width = local_q.shape
    kv_width = local_k.shape[1]
    cached = cache_keys.shape[1]
    head_count = full_width // HEAD_DIM
    kv_heads = kv_width // HEAD_DIM
    hit_limit = hits[0]
    filled = counts[0]
    block_order = assign[0]
    cycle_index = lax.axis_index("blk")
    members = lax.axis_size("blk")
    query_lane = jnp.arange(row_count, dtype=jnp.int32)
    cache_lane = jnp.arange(cached, dtype=jnp.int32)
    own_pos = block_order[cycle_index] * row_count + query_lane
    block_keys = jnp.concatenate([cache_keys[0], local_k], 0)
    block_values = jnp.concatenate([cache_values[0], local_v], 0)

    def allowed_for(block_index, query_pos):
        cache_ok = block_index * cached + cache_lane < hit_limit
        fresh_ok = (block_order[block_index] * row_count + query_lane)[None, :] <= query_pos[
            :, None
        ]
        return jnp.concatenate(
            [jnp.broadcast_to(cache_ok[None, :], (query_pos.shape[0], cached)), fresh_ok], 1
        )

    start = (
        jnp.zeros((row_count, full_width), jnp.float32),
        jnp.full((row_count, head_count), -1e30, jnp.float32),
        jnp.zeros((row_count, head_count), jnp.float32),
    )

    def pass_state(running):
        return shifted(running, "blk", 1)

    def visit_block(visitor, running, turn_index):
        source = (cycle_index - turn_index) % members
        query_pos = block_order[source] * row_count + query_lane
        part = partial_block(
            visitor, block_keys, block_values, allowed_for(cycle_index, query_pos), kv_heads
        )
        return pass_state(combine(running, part, head_count))

    def cycle_turn(turn_index, loop_state):
        visitor, running = loop_state
        running = visit_block(visitor, running, turn_index)
        visitor = shifted(visitor, "blk", 1)
        return (visitor, running)

    visitor, running = lax.fori_loop(0, members - 1, cycle_turn, (local_q, start))
    running = visit_block(visitor, running, members - 1)
    summed, maxima, weights = running
    blended = (summed.reshape(row_count, head_count, -1) / weights[:, :, None]).reshape(
        row_count, full_width
    )
    blended = jnp.where((own_pos < filled)[:, None], blended, 0.0).astype(jnp.bfloat16)
    return lax.all_to_all(blended[None], "grp", split_axis=1, concat_axis=0, tiled=True)


def solution(mesh):
    return jax.shard_map(
        local,
        mesh=mesh,
        in_specs=(
            P(None, ("blk", "grp"), None),
            P("grp", "blk", None),
            P("grp", "blk", None),
            P(None, ("blk", "grp"), None),
            P(None, ("blk", "grp"), None),
            P("grp"),
            P("grp"),
            P("grp", None),
        ),
        out_specs=P(None, ("blk", "grp"), None),
        check_vma=False,
    )
```

profile of v0, /device:TPU:0, one launch (start us, length us, event | category | flops | bytes accessed | tf_op | source)
XLA Modules:
  0.0 164.6 jit_solution(10242938498501873092)
XLA Ops:
  0.0 4.3 %all-to-all-start.1 = ((bf16[4,4,512]{2,1,0:T(4,128)(2,1)}), bf16[4,4,512]{2,1,0:T(4,128)(2,1)S(1)}, u32[]{:S(2)}, u32[]{:S(2)}) async-start(bf16[4,4,512]{2,1,0:T(4,128)(2,1)} %param.13), calls=%async_computation.1 | async-start | bytes 32768 | tf_op jit(solution)/shard_map/all_to_all | solution.py:55
  10.0 3.4 %all-to-all-start.2 = ((bf16[4,4,512]{2,1,0:T(4,128)(2,1)}), bf16[4,4,512]{2,1,0:T(4,128)(2,1)S(1)}, u32[]{:S(2)}, u32[]{:S(2)}) async-start(bf16[4,4,512]{2,1,0:T(4,128)(2,1)} %param.14), calls=%async_computation.2 | async-start | bytes 32768 | tf_op jit(solution)/shard_map/all_to_all | solution.py:56
  13.7 3.7 %all-to-all-done.2 = bf16[4,4,512]{2,1,0:T(4,128)(2,1)S(1)} async-done(((bf16[4,4,512]{2,1,0:T(4,128)(2,1)}), bf16[4,4,512]{2,1,0:T(4,128)(2,1)S(1)}, u32[]{:S(2)}, u32[]{:S(2)}) %all-to-all-start.2) | async-done | bytes 16416 | tf_op jit(solution)/shard_map/all_to_all | solution.py:56
  17.3 3.3 %all-to-all-start = ((bf16[4,4,4096]{2,1,0:T(4,128)(2,1)}), bf16[4,4,4096]{2,1,0:T(4,128)(2,1)S(1)}, u32[]{:S(2)}, u32[]{:S(2)}) async-start(bf16[4,4,4096]{2,1,0:T(4,128)(2,1)} %param.10), calls=%async_computation | async-start | bytes 262144 | tf_op jit(solution)/shard_map/all_to_all | solution.py:54
  21.6 3.7 %all-to-all-done = bf16[4,4,4096]{2,1,0:T(4,128)(2,1)S(1)} async-done(((bf16[4,4,4096]{2,1,0:T(4,128)(2,1)}), bf16[4,4,4096]{2,1,0:T(4,128)(2,1)S(1)}, u32[]{:S(2)}, u32[]{:S(2)}) %all-to-all-start) | async-done | bytes 131104 | tf_op jit(solution)/shard_map/all_to_all | solution.py:54
  25.3 115.3 %while.24 = (s32[]{:T(128)}, bf16[16,4096]{1,0:T(8,128)(2,1)S(1)}, f32[16,4096]{1,0:T(8,128)S(1)}, f32[16,32]{0,1:T(8,128)S(1)}, f32[16,32]{0,1:T(8,128)S(1)}, /...) while((s32[]{:T(128)}, bf16[16,4096]{1,0:T(8,128)(2,1)S(1)}, ...), condition=%wide.wide.region_3.4_spmd.clone.clone, body=%wide.wide.region_0.3_spmd.clone.clone.sunk | while | flops 124177328 | bytes 8742969 | solution.py:109
  29.7 2.0 %collective-permute-start.1 = (f32[16,4096]{1,0:T(8,128)S(1)}, f32[16,4096]{1,0:T(8,128)S(1)}, u32[]{:S(2)}, u32[]{:S(2)}) collective-permute-start(f32[16,4096]{1,0:T(8,128)S(1)} %fusion.72), channel_id=1, source_target_pairs={{0,1},{1,2},{2,3},{3,4},{4,5},{5,6},{6,7},{7,0},{8,9},{9,10},{10,1... | collective-permute-start | bytes 786440 | tf_op jit(solution)/shard_map/while/body/eval_jaxpr/ppermute | solution.py:11
  31.7 1.5 collective-permute-start
  33.3 1.5 collective-permute-start.2
  34.8 1.5 collective-permute-start.3
  36.3 7.7 %collective-permute-done.2 = f32[16,32]{0,1:T(8,128)S(1)} collective-permute-done((f32[16,32]{0,1:T(8,128)S(1)}, f32[16,32]{0,1:T(8,128)S(1)}, u32[]{:S(2)}, u32[]{:S(2)}) %collective-permute-start.2) | collective-permute-done | bytes 2080 | tf_op jit(solution)/shard_map/while/body/eval_jaxpr/ppermute | solution.py:11
  50.4 2.5 %collective-permute-start.3 = (f32[16,32]{0,1:T(8,128)S(1)}, f32[16,32]{0,1:T(8,128)S(1)}, u32[]{:S(2)}, u32[]{:S(2)}) collective-permute-start(f32[16,32]{0,1:T(8,128)S(1)} %get-tuple-element.565), channel_id=1, source_target_pairs={{0,1},{1,2},{2,3},{3,4},{4,5},{5,6},{6,7},{7,0},{8,9},{9,10},{10,1... | collective-permute-start | bytes 6152 | tf_op jit(solution)/shard_map/while/body/eval_jaxpr/ppermute | solution.py:11
  52.8 8.9 %collective-permute-done.2 = f32[16,32]{0,1:T(8,128)S(1)} collective-permute-done((f32[16,32]{0,1:T(8,128)S(1)}, f32[16,32]{0,1:T(8,128)S(1)}, u32[]{:S(2)}, u32[]{:S(2)}) %collective-permute-start.2) | collective-permute-done | bytes 2080 | tf_op jit(solution)/shard_map/while/body/eval_jaxpr/ppermute | solution.py:11
  66.5 2.0 %collective-permute-start.3 = (f32[16,32]{0,1:T(8,128)S(1)}, f32[16,32]{0,1:T(8,128)S(1)}, u32[]{:S(2)}, u32[]{:S(2)}) collective-permute-start(f32[16,32]{0,1:T(8,128)S(1)} %get-tuple-element.565), channel_id=1, source_target_pairs={{0,1},{1,2},{2,3},{3,4},{4,5},{5,6},{6,7},{7,0},{8,9},{9,10},{10,1... | collective-permute-start | bytes 6152 | tf_op jit(solution)/shard_map/while/body/eval_jaxpr/ppermute | solution.py:11
  68.5 10.2 %collective-permute-done.2 = f32[16,32]{0,1:T(8,128)S(1)} collective-permute-done((f32[16,32]{0,1:T(8,128)S(1)}, f32[16,32]{0,1:T(8,128)S(1)}, u32[]{:S(2)}, u32[]{:S(2)}) %collective-permute-start.2) | collective-permute-done | bytes 2080 | tf_op jit(solution)/shard_map/while/body/eval_jaxpr/ppermute | solution.py:11
  83.5 11.2 %collective-permute-done.2 = f32[16,32]{0,1:T(8,128)S(1)} collective-permute-done((f32[16,32]{0,1:T(8,128)S(1)}, f32[16,32]{0,1:T(8,128)S(1)}, u32[]{:S(2)}, u32[]{:S(2)}) %collective-permute-start.2) | collective-permute-done | bytes 2080 | tf_op jit(solution)/shard_map/while/body/eval_jaxpr/ppermute | solution.py:11
  100.0 10.0 %collective-permute-done.2 = f32[16,32]{0,1:T(8,128)S(1)} collective-permute-done((f32[16,32]{0,1:T(8,128)S(1)}, f32[16,32]{0,1:T(8,128)S(1)}, u32[]{:S(2)}, u32[]{:S(2)}) %collective-permute-start.2) | collective-permute-done | bytes 2080 | tf_op jit(solution)/shard_map/while/body/eval_jaxpr/ppermute | solution.py:11
  114.7 1.3 collective-permute-start.3
  116.0 9.2 %collective-permute-done.2 = f32[16,32]{0,1:T(8,128)S(1)} collective-permute-done((f32[16,32]{0,1:T(8,128)S(1)}, f32[16,32]{0,1:T(8,128)S(1)}, u32[]{:S(2)}, u32[]{:S(2)}) %collective-permute-start.2) | collective-permute-done | bytes 2080 | tf_op jit(solution)/shard_map/while/body/eval_jaxpr/ppermute | solution.py:11
  130.0 1.3 collective-permute-start.3
  131.3 9.2 %collective-permute-done.2 = f32[16,32]{0,1:T(8,128)S(1)} collective-permute-done((f32[16,32]{0,1:T(8,128)S(1)}, f32[16,32]{0,1:T(8,128)S(1)}, u32[]{:S(2)}, u32[]{:S(2)}) %collective-permute-start.2) | collective-permute-done | bytes 2080 | tf_op jit(solution)/shard_map/while/body/eval_jaxpr/ppermute | solution.py:11
  143.7 8.5 %collective-permute-done.5 = f32[16,32]{0,1:T(8,128)S(1)} collective-permute-done((f32[16,32]{0,1:T(8,128)S(1)}, f32[16,32]{0,1:T(8,128)S(1)}, u32[]{:S(2)}, u32[]{:S(2)}) %collective-permute-start.5) | collective-permute-done | bytes 2080 | tf_op jit(solution)/shard_map/ppermute | solution.py:11
  153.3 1.4 reduce.2
  154.9 8.2 %all_to_all.19 = bf16[4,2,8192]{2,1,0:T(2,128)(2,1)S(1)} all-to-all(bf16[4,2,8192]{2,1,0:T(2,128)(2,1)S(1)} %reshape.215), channel_id=1, replica_groups=mesh['grp'=4,'blk'=8] {'grp'}, dimensions={0} | all-to-all | bytes 262144 | tf_op jit(solution)/shard_map/all_to_all | solution.py:116
  (243 shorter events, 39.8 us)
Async XLA Ops:
  29.7 14.5 %collective-permute-start.1 = (f32[16,4096]{1,0:T(8,128)S(1)}, f32[16,4096]{1,0:T(8,128)S(1)}, u32[]{:S(2)}, u32[]{:S(2)}) collective-permute-start(f32[16,4096]{1,0:T(8,128)S(1)} %fusion.72), channel_id=1, source_target_pairs={{0,1},{1,2},{2,3},{3,4},{4,5},{5,6},{6,7},{7,0},{8,9},{9,10},{10,1... | collective-permute-start | bytes 786440 | tf_op jit(solution)/shard_map/while/body/eval_jaxpr/ppermute | solution.py:11
  31.7 12.5 %collective-permute-start = (bf16[16,4096]{1,0:T(8,128)(2,1)S(1)}, bf16[16,4096]{1,0:T(8,128)(2,1)S(1)}, u32[]{:S(2)}, u32[]{:S(2)}) collective-permute-start(bf16[16,4096]{1,0:T(8,128)(2,1)S(1)} %copy.144), channel_id=1, source_target_pairs={{0,1},{1,2},{2,3},{3,4},{4,5},{5,6},{6,7},{7,0},{8,9},{9,10},{10,1... | collective-permute-start | bytes 393224 | tf_op jit(solution)/shard_map/while/body/eval_jaxpr/ppermute | solution.py:11
  33.3 10.8 %collective-permute-start.2 = (f32[16,32]{0,1:T(8,128)S(1)}, f32[16,32]{0,1:T(8,128)S(1)}, u32[]{:S(2)}, u32[]{:S(2)}) collective-permute-start(f32[16,32]{0,1:T(8,128)S(1)} %get-tuple-element.564), channel_id=1, source_target_pairs={{0,1},{1,2},{2,3},{3,4},{4,5},{5,6},{6,7},{7,0},{8,9},{9,10},{10,1... | collective-permute-start | bytes 6152 | tf_op jit(solution)/shard_map/while/body/eval_jaxpr/ppermute | solution.py:11
  48.6 13.4 %collective-permute-start.1 = (f32[16,4096]{1,0:T(8,128)S(1)}, f32[16,4096]{1,0:T(8,128)S(1)}, u32[]{:S(2)}, u32[]{:S(2)}) collective-permute-start(f32[16,4096]{1,0:T(8,128)S(1)} %fusion.72), channel_id=1, source_target_pairs={{0,1},{1,2},{2,3},{3,4},{4,5},{5,6},{6,7},{7,0},{8,9},{9,10},{10,1... | collective-permute-start | bytes 786440 | tf_op jit(solution)/shard_map/while/body/eval_jaxpr/ppermute | solution.py:11
  48.7 13.3 %collective-permute-start = (bf16[16,4096]{1,0:T(8,128)(2,1)S(1)}, bf16[16,4096]{1,0:T(8,128)(2,1)S(1)}, u32[]{:S(2)}, u32[]{:S(2)}) collective-permute-start(bf16[16,4096]{1,0:T(8,128)(2,1)S(1)} %copy.144), channel_id=1, source_target_pairs={{0,1},{1,2},{2,3},{3,4},{4,5},{5,6},{6,7},{7,0},{8,9},{9,10},{10,1... | collective-permute-start | bytes 393224 | tf_op jit(solution)/shard_map/while/body/eval_jaxpr/ppermute | solution.py:11
  49.8 12.0 %collective-permute-start.2 = (f32[16,32]{0,1:T(8,128)S(1)}, f32[16,32]{0,1:T(8,128)S(1)}, u32[]{:S(2)}, u32[]{:S(2)}) collective-permute-start(f32[16,32]{0,1:T(8,128)S(1)} %get-tuple-element.564), channel_id=1, source_target_pairs={{0,1},{1,2},{2,3},{3,4},{4,5},{5,6},{6,7},{7,0},{8,9},{9,10},{10,1... | collective-permute-start | bytes 6152 | tf_op jit(solution)/shard_map/while/body/eval_jaxpr/ppermute | solution.py:11
  50.4 11.6 %collective-permute-start.3 = (f32[16,32]{0,1:T(8,128)S(1)}, f32[16,32]{0,1:T(8,128)S(1)}, u32[]{:S(2)}, u32[]{:S(2)}) collective-permute-start(f32[16,32]{0,1:T(8,128)S(1)} %get-tuple-element.565), channel_id=1, source_target_pairs={{0,1},{1,2},{2,3},{3,4},{4,5},{5,6},{6,7},{7,0},{8,9},{9,10},{10,1... | collective-permute-start | bytes 6152 | tf_op jit(solution)/shard_map/while/body/eval_jaxpr/ppermute | solution.py:11
  66.3 12.5 %collective-permute-start.1 = (f32[16,4096]{1,0:T(8,128)S(1)}, f32[16,4096]{1,0:T(8,128)S(1)}, u32[]{:S(2)}, u32[]{:S(2)}) collective-permute-start(f32[16,4096]{1,0:T(8,128)S(1)} %fusion.72), channel_id=1, source_target_pairs={{0,1},{1,2},{2,3},{3,4},{4,5},{5,6},{6,7},{7,0},{8,9},{9,10},{10,1... | collective-permute-start | bytes 786440 | tf_op jit(solution)/shard_map/while/body/eval_jaxpr/ppermute | solution.py:11
  66.4 12.4 %collective-permute-start = (bf16[16,4096]{1,0:T(8,128)(2,1)S(1)}, bf16[16,4096]{1,0:T(8,128)(2,1)S(1)}, u32[]{:S(2)}, u32[]{:S(2)}) collective-permute-start(bf16[16,4096]{1,0:T(8,128)(2,1)S(1)} %copy.144), channel_id=1, source_target_pairs={{0,1},{1,2},{2,3},{3,4},{4,5},{5,6},{6,7},{7,0},{8,9},{9,10},{10,1... | collective-permute-start | bytes 393224 | tf_op jit(solution)/shard_map/while/body/eval_jaxpr/ppermute | solution.py:11
  66.5 12.2 %collective-permute-start.2 = (f32[16,32]{0,1:T(8,128)S(1)}, f32[16,32]{0,1:T(8,128)S(1)}, u32[]{:S(2)}, u32[]{:S(2)}) collective-permute-start(f32[16,32]{0,1:T(8,128)S(1)} %get-tuple-element.564), channel_id=1, source_target_pairs={{0,1},{1,2},{2,3},{3,4},{4,5},{5,6},{6,7},{7,0},{8,9},{9,10},{10,1... | collective-permute-start | bytes 6152 | tf_op jit(solution)/shard_map/while/body/eval_jaxpr/ppermute | solution.py:11
  66.5 12.3 %collective-permute-start.3 = (f32[16,32]{0,1:T(8,128)S(1)}, f32[16,32]{0,1:T(8,128)S(1)}, u32[]{:S(2)}, u32[]{:S(2)}) collective-permute-start(f32[16,32]{0,1:T(8,128)S(1)} %get-tuple-element.565), channel_id=1, source_target_pairs={{0,1},{1,2},{2,3},{3,4},{4,5},{5,6},{6,7},{7,0},{8,9},{9,10},{10,1... | collective-permute-start | bytes 6152 | tf_op jit(solution)/shard_map/while/body/eval_jaxpr/ppermute | solution.py:11
  83.2 11.7 %collective-permute-start.1 = (f32[16,4096]{1,0:T(8,128)S(1)}, f32[16,4096]{1,0:T(8,128)S(1)}, u32[]{:S(2)}, u32[]{:S(2)}) collective-permute-start(f32[16,4096]{1,0:T(8,128)S(1)} %fusion.72), channel_id=1, source_target_pairs={{0,1},{1,2},{2,3},{3,4},{4,5},{5,6},{6,7},{7,0},{8,9},{9,10},{10,1... | collective-permute-start | bytes 786440 | tf_op jit(solution)/shard_map/while/body/eval_jaxpr/ppermute | solution.py:11
  83.3 11.6 %collective-permute-start = (bf16[16,4096]{1,0:T(8,128)(2,1)S(1)}, bf16[16,4096]{1,0:T(8,128)(2,1)S(1)}, u32[]{:S(2)}, u32[]{:S(2)}) collective-permute-start(bf16[16,4096]{1,0:T(8,128)(2,1)S(1)} %copy.144), channel_id=1, source_target_pairs={{0,1},{1,2},{2,3},{3,4},{4,5},{5,6},{6,7},{7,0},{8,9},{9,10},{10,1... | collective-permute-start | bytes 393224 | tf_op jit(solution)/shard_map/while/body/eval_jaxpr/ppermute | solution.py:11
  83.4 11.4 %collective-permute-start.2 = (f32[16,32]{0,1:T(8,128)S(1)}, f32[16,32]{0,1:T(8,128)S(1)}, u32[]{:S(2)}, u32[]{:S(2)}) collective-permute-start(f32[16,32]{0,1:T(8,128)S(1)} %get-tuple-element.564), channel_id=1, source_target_pairs={{0,1},{1,2},{2,3},{3,4},{4,5},{5,6},{6,7},{7,0},{8,9},{9,10},{10,1... | collective-permute-start | bytes 6152 | tf_op jit(solution)/shard_map/while/body/eval_jaxpr/ppermute | solution.py:11
  83.4 11.5 %collective-permute-start.3 = (f32[16,32]{0,1:T(8,128)S(1)}, f32[16,32]{0,1:T(8,128)S(1)}, u32[]{:S(2)}, u32[]{:S(2)}) collective-permute-start(f32[16,32]{0,1:T(8,128)S(1)} %get-tuple-element.565), channel_id=1, source_target_pairs={{0,1},{1,2},{2,3},{3,4},{4,5},{5,6},{6,7},{7,0},{8,9},{9,10},{10,1... | collective-permute-start | bytes 6152 | tf_op jit(solution)/shard_map/while/body/eval_jaxpr/ppermute | solution.py:11
  99.3 10.9 %collective-permute-start.1 = (f32[16,4096]{1,0:T(8,128)S(1)}, f32[16,4096]{1,0:T(8,128)S(1)}, u32[]{:S(2)}, u32[]{:S(2)}) collective-permute-start(f32[16,4096]{1,0:T(8,128)S(1)} %fusion.72), channel_id=1, source_target_pairs={{0,1},{1,2},{2,3},{3,4},{4,5},{5,6},{6,7},{7,0},{8,9},{9,10},{10,1... | collective-permute-start | bytes 786440 | tf_op jit(solution)/shard_map/while/body/eval_jaxpr/ppermute | solution.py:11
  99.3 10.8 %collective-permute-start = (bf16[16,4096]{1,0:T(8,128)(2,1)S(1)}, bf16[16,4096]{1,0:T(8,128)(2,1)S(1)}, u32[]{:S(2)}, u32[]{:S(2)}) collective-permute-start(bf16[16,4096]{1,0:T(8,128)(2,1)S(1)} %copy.144), channel_id=1, source_target_pairs={{0,1},{1,2},{2,3},{3,4},{4,5},{5,6},{6,7},{7,0},{8,9},{9,10},{10,1... | collective-permute-start | bytes 393224 | tf_op jit(solution)/shard_map/while/body/eval_jaxpr/ppermute | solution.py:11
  99.5 10.7 %collective-permute-start.3 = (f32[16,32]{0,1:T(8,128)S(1)}, f32[16,32]{0,1:T(8,128)S(1)}, u32[]{:S(2)}, u32[]{:S(2)}) collective-permute-start(f32[16,32]{0,1:T(8,128)S(1)} %get-tuple-element.565), channel_id=1, source_target_pairs={{0,1},{1,2},{2,3},{3,4},{4,5},{5,6},{6,7},{7,0},{8,9},{9,10},{10,1... | collective-permute-start | bytes 6152 | tf_op jit(solution)/shard_map/while/body/eval_jaxpr/ppermute | solution.py:11
  114.5 10.9 %collective-permute-start.1 = (f32[16,4096]{1,0:T(8,128)S(1)}, f32[16,4096]{1,0:T(8,128)S(1)}, u32[]{:S(2)}, u32[]{:S(2)}) collective-permute-start(f32[16,4096]{1,0:T(8,128)S(1)} %fusion.72), channel_id=1, source_target_pairs={{0,1},{1,2},{2,3},{3,4},{4,5},{5,6},{6,7},{7,0},{8,9},{9,10},{10,1... | collective-permute-start | bytes 786440 | tf_op jit(solution)/shard_map/while/body/eval_jaxpr/ppermute | solution.py:11
  114.6 10.8 %collective-permute-start = (bf16[16,4096]{1,0:T(8,128)(2,1)S(1)}, bf16[16,4096]{1,0:T(8,128)(2,1)S(1)}, u32[]{:S(2)}, u32[]{:S(2)}) collective-permute-start(bf16[16,4096]{1,0:T(8,128)(2,1)S(1)} %copy.144), channel_id=1, source_target_pairs={{0,1},{1,2},{2,3},{3,4},{4,5},{5,6},{6,7},{7,0},{8,9},{9,10},{10,1... | collective-permute-start | bytes 393224 | tf_op jit(solution)/shard_map/while/body/eval_jaxpr/ppermute | solution.py:11
  114.7 10.7 %collective-permute-start.3 = (f32[16,32]{0,1:T(8,128)S(1)}, f32[16,32]{0,1:T(8,128)S(1)}, u32[]{:S(2)}, u32[]{:S(2)}) collective-permute-start(f32[16,32]{0,1:T(8,128)S(1)} %get-tuple-element.565), channel_id=1, source_target_pairs={{0,1},{1,2},{2,3},{3,4},{4,5},{5,6},{6,7},{7,0},{8,9},{9,10},{10,1... | collective-permute-start | bytes 6152 | tf_op jit(solution)/shard_map/while/body/eval_jaxpr/ppermute | solution.py:11
  129.8 10.9 %collective-permute-start.1 = (f32[16,4096]{1,0:T(8,128)S(1)}, f32[16,4096]{1,0:T(8,128)S(1)}, u32[]{:S(2)}, u32[]{:S(2)}) collective-permute-start(f32[16,4096]{1,0:T(8,128)S(1)} %fusion.72), channel_id=1, source_target_pairs={{0,1},{1,2},{2,3},{3,4},{4,5},{5,6},{6,7},{7,0},{8,9},{9,10},{10,1... | collective-permute-start | bytes 786440 | tf_op jit(solution)/shard_map/while/body/eval_jaxpr/ppermute | solution.py:11
  129.9 10.8 %collective-permute-start = (bf16[16,4096]{1,0:T(8,128)(2,1)S(1)}, bf16[16,4096]{1,0:T(8,128)(2,1)S(1)}, u32[]{:S(2)}, u32[]{:S(2)}) collective-permute-start(bf16[16,4096]{1,0:T(8,128)(2,1)S(1)} %copy.144), channel_id=1, source_target_pairs={{0,1},{1,2},{2,3},{3,4},{4,5},{5,6},{6,7},{7,0},{8,9},{9,10},{10,1... | collective-permute-start | bytes 393224 | tf_op jit(solution)/shard_map/while/body/eval_jaxpr/ppermute | solution.py:11
  130.0 10.7 %collective-permute-start.3 = (f32[16,32]{0,1:T(8,128)S(1)}, f32[16,32]{0,1:T(8,128)S(1)}, u32[]{:S(2)}, u32[]{:S(2)}) collective-permute-start(f32[16,32]{0,1:T(8,128)S(1)} %get-tuple-element.565), channel_id=1, source_target_pairs={{0,1},{1,2},{2,3},{3,4},{4,5},{5,6},{6,7},{7,0},{8,9},{9,10},{10,1... | collective-permute-start | bytes 6152 | tf_op jit(solution)/shard_map/while/body/eval_jaxpr/ppermute | solution.py:11
  (15 other events, 209.6 us)
where the time goes:
time: 165 us
  waiting for transfers between devices  83.6 us (51%)
  starting transfers between devices  27.9 us (17%)
  local copies, waits for them, and re-layouts  16 us (10%)
  other arithmetic  14 us (8%)
  blocking collectives  8.17 us (5%)
  matrix products  6.6 us (4%)
  loops' own time  5.46 us (3%)
  between operations  2.83 us (2%)
    ppermute x30, waiting for transfers between devices, shifted(): lax.ppermute(value, axis, [(i, (i + by) % length) for i in range(length)])  76.3 us
    ppermute x30, starting transfers between devices, shifted(): lax.ppermute(value, axis, [(i, (i + by) % length) for i in range(length)])  16.9 us
    all_to_all x1, blocking collectives, local(): lax.all_to_all(blended[None], 'grp', split_axis=1, concat_axis=0, tiled=T...  8.17 us
    another operation x1, loops' own time, local(): lax.fori_loop(0, members - 1, cycle_turn, (local_q, start))  5.46 us
    dynamic_slice x8, local copies, waits for them, and re-layouts, visit_block(): query_pos = block_order[source] * row_count + query_lane  5.17 us
    lt x8, other arithmetic, allowed_for(): cache_ok = block_index * cached + cache_lane < hit_limit  4.57 us
    all_to_all x1, starting transfers between devices, local(): lax.all_to_all(new_keys, 'grp', split_axis=0, concat_axis=1, tiled=True)  4.26 us
    all_to_all x1, waiting for transfers between devices, local(): lax.all_to_all(queries, 'grp', split_axis=0, concat_axis=1, tiled=True)  3.68 us
  transfers between devices with their start and end apart: 33, of which 17 were waited for; matrix products, arithmetic and copies ran while one was open for 2% of the time, Pallas kernels for 0%

commit v1 on v0

--- a/solution.py
+++ b/solution.py
@@ -2,8 +2,17 @@
 import jax.numpy as jnp
 from jax import lax
 from jax.sharding import PartitionSpec as P
+from jax.lax import all_to_all, axis_size
 
 HEAD_DIM = 128
+
+
+def treat_frames(vec):
+    val = axis_size("grp")
+    inter = jnp.split(vec, val, 1)
+    block_now = jnp.stack(inter)
+    odd = all_to_all(block_now, "grp", 0, 0)
+    return jnp.concatenate(odd, 0)
 
 
 def shifted(value, axis, by):
@@ -113,7 +122,7 @@
         row_count, full_width
     )
     blended = jnp.where((own_pos < filled)[:, None], blended, 0.0).astype(jnp.bfloat16)
-    return lax.all_to_all(blended[None], "grp", split_axis=1, concat_axis=0, tiled=True)
+    return treat_frames(blended[None])
 
 
 def solution(mesh):

time: 165 us -> 162 us (0.982)
  local copies, waits for them, and re-layouts: 16 us -> 14 us
where the time goes in v1:
time: 162 us; the launch traced here: 161 us
  waiting for transfers between devices  83.6 us (52%)
  starting transfers between devices  27.9 us (17%)
  local copies, waits for them, and re-layouts  14 us (9%)
  other arithmetic  12.7 us (8%)
  blocking collectives  8.2 us (5%)
  matrix products  6.61 us (4%)
  loops' own time  5.44 us (3%)
  between operations  2.89 us (2%)
    ppermute x30, waiting for transfers between devices, shifted(): lax.ppermute(value, axis, [(i, (i + by) % length) for i in range(length)])  76.2 us
    ppermute x30, starting transfers between devices, shifted(): lax.ppermute(value, axis, [(i, (i + by) % length) for i in range(length)])  16.9 us
    all_to_all x1, blocking collectives, treat_frames(): odd = all_to_all(block_now, 'grp', 0, 0)  8.2 us
    another operation x1, loops' own time, local(): lax.fori_loop(0, members - 1, cycle_turn, (local_q, start))  5.44 us
    dynamic_slice x8, local copies, waits for them, and re-layouts, visit_block(): query_pos = block_order[source] * row_count + query_lane  4.91 us
    lt x8, other arithmetic, allowed_for(): cache_ok = block_index * cached + cache_lane < hit_limit  4.57 us
    all_to_all x1, starting transfers between devices, local(): lax.all_to_all(new_keys, 'grp', split_axis=0, concat_axis=1, tiled=True)  4.26 us
    all_to_all x1, waiting for transfers between devices, local(): lax.all_to_all(queries, 'grp', split_axis=0, concat_axis=1, tiled=True)  3.68 us
  transfers between devices with their start and end apart: 33, of which 17 were waited for; matrix products, arithmetic and copies ran while one was open for 2% of the time, Pallas kernels for 0%

profile of v1, /device:TPU:0, one launch (start us, length us, event | category | flops | bytes accessed | tf_op | source)
XLA Modules:
  0.0 161.4 jit_solution(6893438910517770208)
XLA Ops:
  0.0 4.3 %all-to-all-start.1 = ((bf16[4,4,512]{2,1,0:T(4,128)(2,1)}), bf16[4,4,512]{2,1,0:T(4,128)(2,1)S(1)}, u32[]{:S(2)}, u32[]{:S(2)}) async-start(bf16[4,4,512]{2,1,0:T(4,128)(2,1)} %param.13), calls=%async_computation.1 | async-start | bytes 32768 | tf_op jit(solution)/shard_map/all_to_all | solution.py:64
  10.1 3.4 %all-to-all-start.2 = ((bf16[4,4,512]{2,1,0:T(4,128)(2,1)}), bf16[4,4,512]{2,1,0:T(4,128)(2,1)S(1)}, u32[]{:S(2)}, u32[]{:S(2)}) async-start(bf16[4,4,512]{2,1,0:T(4,128)(2,1)} %param.14), calls=%async_computation.2 | async-start | bytes 32768 | tf_op jit(solution)/shard_map/all_to_all | solution.py:65
  13.8 3.7 %all-to-all-done.2 = bf16[4,4,512]{2,1,0:T(4,128)(2,1)S(1)} async-done(((bf16[4,4,512]{2,1,0:T(4,128)(2,1)}), bf16[4,4,512]{2,1,0:T(4,128)(2,1)S(1)}, u32[]{:S(2)}, u32[]{:S(2)}) %all-to-all-start.2) | async-done | bytes 16416 | tf_op jit(solution)/shard_map/all_to_all | solution.py:65
  17.4 3.3 %all-to-all-start = ((bf16[4,4,4096]{2,1,0:T(4,128)(2,1)}), bf16[4,4,4096]{2,1,0:T(4,128)(2,1)S(1)}, u32[]{:S(2)}, u32[]{:S(2)}) async-start(bf16[4,4,4096]{2,1,0:T(4,128)(2,1)} %param.10), calls=%async_computation | async-start | bytes 262144 | tf_op jit(solution)/shard_map/all_to_all | solution.py:63
  21.7 3.7 %all-to-all-done = bf16[4,4,4096]{2,1,0:T(4,128)(2,1)S(1)} async-done(((bf16[4,4,4096]{2,1,0:T(4,128)(2,1)}), bf16[4,4,4096]{2,1,0:T(4,128)(2,1)S(1)}, u32[]{:S(2)}, u32[]{:S(2)}) %all-to-all-start) | async-done | bytes 131104 | tf_op jit(solution)/shard_map/all_to_all | solution.py:63
  25.4 115.0 %while.24 = (s32[]{:T(128)}, bf16[16,4096]{1,0:T(8,128)(2,1)S(1)}, f32[16,4096]{1,0:T(8,128)S(1)}, f32[16,32]{0,1:T(8,128)S(1)}, f32[16,32]{0,1:T(8,128)S(1)}, /...) while((s32[]{:T(128)}, bf16[16,4096]{1,0:T(8,128)(2,1)S(1)}, ...), condition=%wide.wide.region_3.4_spmd.clone.clone, body=%wide.wide.region_0.3_spmd.clone.clone.sunk | while | flops 124177328 | bytes 8742969 | solution.py:118
  29.8 2.0 %collective-permute-start.1 = (f32[16,4096]{1,0:T(8,128)S(1)}, f32[16,4096]{1,0:T(8,128)S(1)}, u32[]{:S(2)}, u32[]{:S(2)}) collective-permute-start(f32[16,4096]{1,0:T(8,128)S(1)} %fusion.72), channel_id=1, source_target_pairs={{0,1},{1,2},{2,3},{3,4},{4,5},{5,6},{6,7},{7,0},{8,9},{9,10},{10,1... | collective-permute-start | bytes 786440 | tf_op jit(solution)/shard_map/while/body/eval_jaxpr/ppermute | solution.py:20
  31.8 1.6 collective-permute-start
  33.3 1.5 collective-permute-start.2
  34.8 1.6 collective-permute-start.3
  36.4 7.7 %collective-permute-done.2 = f32[16,32]{0,1:T(8,128)S(1)} collective-permute-done((f32[16,32]{0,1:T(8,128)S(1)}, f32[16,32]{0,1:T(8,128)S(1)}, u32[]{:S(2)}, u32[]{:S(2)}) %collective-permute-start.2) | collective-permute-done | bytes 2080 | tf_op jit(solution)/shard_map/while/body/eval_jaxpr/ppermute | solution.py:20
  48.7 1.1 collective-permute-start
  50.4 2.4 %collective-permute-start.3 = (f32[16,32]{0,1:T(8,128)S(1)}, f32[16,32]{0,1:T(8,128)S(1)}, u32[]{:S(2)}, u32[]{:S(2)}) collective-permute-start(f32[16,32]{0,1:T(8,128)S(1)} %get-tuple-element.569), channel_id=1, source_target_pairs={{0,1},{1,2},{2,3},{3,4},{4,5},{5,6},{6,7},{7,0},{8,9},{9,10},{10,1... | collective-permute-start | bytes 6152 | tf_op jit(solution)/shard_map/while/body/eval_jaxpr/ppermute | solution.py:20
  52.9 8.9 %collective-permute-done.2 = f32[16,32]{0,1:T(8,128)S(1)} collective-permute-done((f32[16,32]{0,1:T(8,128)S(1)}, f32[16,32]{0,1:T(8,128)S(1)}, u32[]{:S(2)}, u32[]{:S(2)}) %collective-permute-start.2) | collective-permute-done | bytes 2080 | tf_op jit(solution)/shard_map/while/body/eval_jaxpr/ppermute | solution.py:20
  66.5 2.0 %collective-permute-start.3 = (f32[16,32]{0,1:T(8,128)S(1)}, f32[16,32]{0,1:T(8,128)S(1)}, u32[]{:S(2)}, u32[]{:S(2)}) collective-permute-start(f32[16,32]{0,1:T(8,128)S(1)} %get-tuple-element.569), channel_id=1, source_target_pairs={{0,1},{1,2},{2,3},{3,4},{4,5},{5,6},{6,7},{7,0},{8,9},{9,10},{10,1... | collective-permute-start | bytes 6152 | tf_op jit(solution)/shard_map/while/body/eval_jaxpr/ppermute | solution.py:20
  68.5 10.2 %collective-permute-done.2 = f32[16,32]{0,1:T(8,128)S(1)} collective-permute-done((f32[16,32]{0,1:T(8,128)S(1)}, f32[16,32]{0,1:T(8,128)S(1)}, u32[]{:S(2)}, u32[]{:S(2)}) %collective-permute-start.2) | collective-permute-done | bytes 2080 | tf_op jit(solution)/shard_map/while/body/eval_jaxpr/ppermute | solution.py:20
  83.4 11.2 %collective-permute-done.2 = f32[16,32]{0,1:T(8,128)S(1)} collective-permute-done((f32[16,32]{0,1:T(8,128)S(1)}, f32[16,32]{0,1:T(8,128)S(1)}, u32[]{:S(2)}, u32[]{:S(2)}) %collective-permute-start.2) | collective-permute-done | bytes 2080 | tf_op jit(solution)/shard_map/while/body/eval_jaxpr/ppermute | solution.py:20
  99.8 10.0 %collective-permute-done.2 = f32[16,32]{0,1:T(8,128)S(1)} collective-permute-done((f32[16,32]{0,1:T(8,128)S(1)}, f32[16,32]{0,1:T(8,128)S(1)}, u32[]{:S(2)}, u32[]{:S(2)}) %collective-permute-start.2) | collective-permute-done | bytes 2080 | tf_op jit(solution)/shard_map/while/body/eval_jaxpr/ppermute | solution.py:20
  114.6 1.3 collective-permute-start.3
  115.8 9.2 %collective-permute-done.2 = f32[16,32]{0,1:T(8,128)S(1)} collective-permute-done((f32[16,32]{0,1:T(8,128)S(1)}, f32[16,32]{0,1:T(8,128)S(1)}, u32[]{:S(2)}, u32[]{:S(2)}) %collective-permute-start.2) | collective-permute-done | bytes 2080 | tf_op jit(solution)/shard_map/while/body/eval_jaxpr/ppermute | solution.py:20
  129.8 1.3 collective-permute-start.3
  131.1 9.2 %collective-permute-done.2 = f32[16,32]{0,1:T(8,128)S(1)} collective-permute-done((f32[16,32]{0,1:T(8,128)S(1)}, f32[16,32]{0,1:T(8,128)S(1)}, u32[]{:S(2)}, u32[]{:S(2)}) %collective-permute-start.2) | collective-permute-done | bytes 2080 | tf_op jit(solution)/shard_map/while/body/eval_jaxpr/ppermute | solution.py:20
  143.4 8.5 %collective-permute-done.5 = f32[16,32]{0,1:T(8,128)S(1)} collective-permute-done((f32[16,32]{0,1:T(8,128)S(1)}, f32[16,32]{0,1:T(8,128)S(1)}, u32[]{:S(2)}, u32[]{:S(2)}) %collective-permute-start.5) | collective-permute-done | bytes 2080 | tf_op jit(solution)/shard_map/ppermute | solution.py:20
  152.5 8.2 %all_to_all.32 = bf16[4,1,4,4096]{3,2,1,0:T(4,128)(2,1)S(1)} all-to-all(bf16[4,1,4,4096]{3,2,1,0:T(4,128)(2,1)S(1)} %pad_maximum_fusion.2), channel_id=1, replica_groups=mesh['grp'=4,'blk'=8] {'grp'}, dimensions={0} | all-to-all | bytes 262144 | tf_op jit(solution)/shard_map/all_to_all | solution.py:14
  (239 shorter events, 36.8 us)
Async XLA Ops:
  29.8 14.5 %collective-permute-start.1 = (f32[16,4096]{1,0:T(8,128)S(1)}, f32[16,4096]{1,0:T(8,128)S(1)}, u32[]{:S(2)}, u32[]{:S(2)}) collective-permute-start(f32[16,4096]{1,0:T(8,128)S(1)} %fusion.72), channel_id=1, source_target_pairs={{0,1},{1,2},{2,3},{3,4},{4,5},{5,6},{6,7},{7,0},{8,9},{9,10},{10,1... | collective-permute-start | bytes 786440 | tf_op jit(solution)/shard_map/while/body/eval_jaxpr/ppermute | solution.py:20
  31.8 12.5 %collective-permute-start = (bf16[16,4096]{1,0:T(8,128)(2,1)S(1)}, bf16[16,4096]{1,0:T(8,128)(2,1)S(1)}, u32[]{:S(2)}, u32[]{:S(2)}) collective-permute-start(bf16[16,4096]{1,0:T(8,128)(2,1)S(1)} %copy.112), channel_id=1, source_target_pairs={{0,1},{1,2},{2,3},{3,4},{4,5},{5,6},{6,7},{7,0},{8,9},{9,10},{10,1... | collective-permute-start | bytes 393224 | tf_op jit(solution)/shard_map/while/body/eval_jaxpr/ppermute | solution.py:20
  33.3 10.8 %collective-permute-start.2 = (f32[16,32]{0,1:T(8,128)S(1)}, f32[16,32]{0,1:T(8,128)S(1)}, u32[]{:S(2)}, u32[]{:S(2)}) collective-permute-start(f32[16,32]{0,1:T(8,128)S(1)} %get-tuple-element.568), channel_id=1, source_target_pairs={{0,1},{1,2},{2,3},{3,4},{4,5},{5,6},{6,7},{7,0},{8,9},{9,10},{10,1... | collective-permute-start | bytes 6152 | tf_op jit(solution)/shard_map/while/body/eval_jaxpr/ppermute | solution.py:20
  48.6 13.4 %collective-permute-start.1 = (f32[16,4096]{1,0:T(8,128)S(1)}, f32[16,4096]{1,0:T(8,128)S(1)}, u32[]{:S(2)}, u32[]{:S(2)}) collective-permute-start(f32[16,4096]{1,0:T(8,128)S(1)} %fusion.72), channel_id=1, source_target_pairs={{0,1},{1,2},{2,3},{3,4},{4,5},{5,6},{6,7},{7,0},{8,9},{9,10},{10,1... | collective-permute-start | bytes 786440 | tf_op jit(solution)/shard_map/while/body/eval_jaxpr/ppermute | solution.py:20
  48.7 13.3 %collective-permute-start = (bf16[16,4096]{1,0:T(8,128)(2,1)S(1)}, bf16[16,4096]{1,0:T(8,128)(2,1)S(1)}, u32[]{:S(2)}, u32[]{:S(2)}) collective-permute-start(bf16[16,4096]{1,0:T(8,128)(2,1)S(1)} %copy.112), channel_id=1, source_target_pairs={{0,1},{1,2},{2,3},{3,4},{4,5},{5,6},{6,7},{7,0},{8,9},{9,10},{10,1... | collective-permute-start | bytes 393224 | tf_op jit(solution)/shard_map/while/body/eval_jaxpr/ppermute | solution.py:20
  49.8 12.0 %collective-permute-start.2 = (f32[16,32]{0,1:T(8,128)S(1)}, f32[16,32]{0,1:T(8,128)S(1)}, u32[]{:S(2)}, u32[]{:S(2)}) collective-permute-start(f32[16,32]{0,1:T(8,128)S(1)} %get-tuple-element.568), channel_id=1, source_target_pairs={{0,1},{1,2},{2,3},{3,4},{4,5},{5,6},{6,7},{7,0},{8,9},{9,10},{10,1... | collective-permute-start | bytes 6152 | tf_op jit(solution)/shard_map/while/body/eval_jaxpr/ppermute | solution.py:20
  50.4 11.6 %collective-permute-start.3 = (f32[16,32]{0,1:T(8,128)S(1)}, f32[16,32]{0,1:T(8,128)S(1)}, u32[]{:S(2)}, u32[]{:S(2)}) collective-permute-start(f32[16,32]{0,1:T(8,128)S(1)} %get-tuple-element.569), channel_id=1, source_target_pairs={{0,1},{1,2},{2,3},{3,4},{4,5},{5,6},{6,7},{7,0},{8,9},{9,10},{10,1... | collective-permute-start | bytes 6152 | tf_op jit(solution)/shard_map/while/body/eval_jaxpr/ppermute | solution.py:20
  66.3 12.5 %collective-permute-start.1 = (f32[16,4096]{1,0:T(8,128)S(1)}, f32[16,4096]{1,0:T(8,128)S(1)}, u32[]{:S(2)}, u32[]{:S(2)}) collective-permute-start(f32[16,4096]{1,0:T(8,128)S(1)} %fusion.72), channel_id=1, source_target_pairs={{0,1},{1,2},{2,3},{3,4},{4,5},{5,6},{6,7},{7,0},{8,9},{9,10},{10,1... | collective-permute-start | bytes 786440 | tf_op jit(solution)/shard_map/while/body/eval_jaxpr/ppermute | solution.py:20
  66.4 12.4 %collective-permute-start = (bf16[16,4096]{1,0:T(8,128)(2,1)S(1)}, bf16[16,4096]{1,0:T(8,128)(2,1)S(1)}, u32[]{:S(2)}, u32[]{:S(2)}) collective-permute-start(bf16[16,4096]{1,0:T(8,128)(2,1)S(1)} %copy.112), channel_id=1, source_target_pairs={{0,1},{1,2},{2,3},{3,4},{4,5},{5,6},{6,7},{7,0},{8,9},{9,10},{10,1... | collective-permute-start | bytes 393224 | tf_op jit(solution)/shard_map/while/body/eval_jaxpr/ppermute | solution.py:20
  66.4 12.2 %collective-permute-start.2 = (f32[16,32]{0,1:T(8,128)S(1)}, f32[16,32]{0,1:T(8,128)S(1)}, u32[]{:S(2)}, u32[]{:S(2)}) collective-permute-start(f32[16,32]{0,1:T(8,128)S(1)} %get-tuple-element.568), channel_id=1, source_target_pairs={{0,1},{1,2},{2,3},{3,4},{4,5},{5,6},{6,7},{7,0},{8,9},{9,10},{10,1... | collective-permute-start | bytes 6152 | tf_op jit(solution)/shard_map/while/body/eval_jaxpr/ppermute | solution.py:20
  66.5 12.3 %collective-permute-start.3 = (f32[16,32]{0,1:T(8,128)S(1)}, f32[16,32]{0,1:T(8,128)S(1)}, u32[]{:S(2)}, u32[]{:S(2)}) collective-permute-start(f32[16,32]{0,1:T(8,128)S(1)} %get-tuple-element.569), channel_id=1, source_target_pairs={{0,1},{1,2},{2,3},{3,4},{4,5},{5,6},{6,7},{7,0},{8,9},{9,10},{10,1... | collective-permute-start | bytes 6152 | tf_op jit(solution)/shard_map/while/body/eval_jaxpr/ppermute | solution.py:20
  83.2 11.6 %collective-permute-start.1 = (f32[16,4096]{1,0:T(8,128)S(1)}, f32[16,4096]{1,0:T(8,128)S(1)}, u32[]{:S(2)}, u32[]{:S(2)}) collective-permute-start(f32[16,4096]{1,0:T(8,128)S(1)} %fusion.72), channel_id=1, source_target_pairs={{0,1},{1,2},{2,3},{3,4},{4,5},{5,6},{6,7},{7,0},{8,9},{9,10},{10,1... | collective-permute-start | bytes 786440 | tf_op jit(solution)/shard_map/while/body/eval_jaxpr/ppermute | solution.py:20
  83.2 11.6 %collective-permute-start = (bf16[16,4096]{1,0:T(8,128)(2,1)S(1)}, bf16[16,4096]{1,0:T(8,128)(2,1)S(1)}, u32[]{:S(2)}, u32[]{:S(2)}) collective-permute-start(bf16[16,4096]{1,0:T(8,128)(2,1)S(1)} %copy.112), channel_id=1, source_target_pairs={{0,1},{1,2},{2,3},{3,4},{4,5},{5,6},{6,7},{7,0},{8,9},{9,10},{10,1... | collective-permute-start | bytes 393224 | tf_op jit(solution)/shard_map/while/body/eval_jaxpr/ppermute | solution.py:20
  83.3 11.3 %collective-permute-start.2 = (f32[16,32]{0,1:T(8,128)S(1)}, f32[16,32]{0,1:T(8,128)S(1)}, u32[]{:S(2)}, u32[]{:S(2)}) collective-permute-start(f32[16,32]{0,1:T(8,128)S(1)} %get-tuple-element.568), channel_id=1, source_target_pairs={{0,1},{1,2},{2,3},{3,4},{4,5},{5,6},{6,7},{7,0},{8,9},{9,10},{10,1... | collective-permute-start | bytes 6152 | tf_op jit(solution)/shard_map/while/body/eval_jaxpr/ppermute | solution.py:20
  83.4 11.4 %collective-permute-start.3 = (f32[16,32]{0,1:T(8,128)S(1)}, f32[16,32]{0,1:T(8,128)S(1)}, u32[]{:S(2)}, u32[]{:S(2)}) collective-permute-start(f32[16,32]{0,1:T(8,128)S(1)} %get-tuple-element.569), channel_id=1, source_target_pairs={{0,1},{1,2},{2,3},{3,4},{4,5},{5,6},{6,7},{7,0},{8,9},{9,10},{10,1... | collective-permute-start | bytes 6152 | tf_op jit(solution)/shard_map/while/body/eval_jaxpr/ppermute | solution.py:20
  99.1 10.9 %collective-permute-start.1 = (f32[16,4096]{1,0:T(8,128)S(1)}, f32[16,4096]{1,0:T(8,128)S(1)}, u32[]{:S(2)}, u32[]{:S(2)}) collective-permute-start(f32[16,4096]{1,0:T(8,128)S(1)} %fusion.72), channel_id=1, source_target_pairs={{0,1},{1,2},{2,3},{3,4},{4,5},{5,6},{6,7},{7,0},{8,9},{9,10},{10,1... | collective-permute-start | bytes 786440 | tf_op jit(solution)/shard_map/while/body/eval_jaxpr/ppermute | solution.py:20
  99.2 10.8 %collective-permute-start = (bf16[16,4096]{1,0:T(8,128)(2,1)S(1)}, bf16[16,4096]{1,0:T(8,128)(2,1)S(1)}, u32[]{:S(2)}, u32[]{:S(2)}) collective-permute-start(bf16[16,4096]{1,0:T(8,128)(2,1)S(1)} %copy.112), channel_id=1, source_target_pairs={{0,1},{1,2},{2,3},{3,4},{4,5},{5,6},{6,7},{7,0},{8,9},{9,10},{10,1... | collective-permute-start | bytes 393224 | tf_op jit(solution)/shard_map/while/body/eval_jaxpr/ppermute | solution.py:20
  99.3 10.7 %collective-permute-start.3 = (f32[16,32]{0,1:T(8,128)S(1)}, f32[16,32]{0,1:T(8,128)S(1)}, u32[]{:S(2)}, u32[]{:S(2)}) collective-permute-start(f32[16,32]{0,1:T(8,128)S(1)} %get-tuple-element.569), channel_id=1, source_target_pairs={{0,1},{1,2},{2,3},{3,4},{4,5},{5,6},{6,7},{7,0},{8,9},{9,10},{10,1... | collective-permute-start | bytes 6152 | tf_op jit(solution)/shard_map/while/body/eval_jaxpr/ppermute | solution.py:20
  114.4 10.9 %collective-permute-start.1 = (f32[16,4096]{1,0:T(8,128)S(1)}, f32[16,4096]{1,0:T(8,128)S(1)}, u32[]{:S(2)}, u32[]{:S(2)}) collective-permute-start(f32[16,4096]{1,0:T(8,128)S(1)} %fusion.72), channel_id=1, source_target_pairs={{0,1},{1,2},{2,3},{3,4},{4,5},{5,6},{6,7},{7,0},{8,9},{9,10},{10,1... | collective-permute-start | bytes 786440 | tf_op jit(solution)/shard_map/while/body/eval_jaxpr/ppermute | solution.py:20
  114.4 10.8 %collective-permute-start = (bf16[16,4096]{1,0:T(8,128)(2,1)S(1)}, bf16[16,4096]{1,0:T(8,128)(2,1)S(1)}, u32[]{:S(2)}, u32[]{:S(2)}) collective-permute-start(bf16[16,4096]{1,0:T(8,128)(2,1)S(1)} %copy.112), channel_id=1, source_target_pairs={{0,1},{1,2},{2,3},{3,4},{4,5},{5,6},{6,7},{7,0},{8,9},{9,10},{10,1... | collective-permute-start | bytes 393224 | tf_op jit(solution)/shard_map/while/body/eval_jaxpr/ppermute | solution.py:20
  114.6 10.7 %collective-permute-start.3 = (f32[16,32]{0,1:T(8,128)S(1)}, f32[16,32]{0,1:T(8,128)S(1)}, u32[]{:S(2)}, u32[]{:S(2)}) collective-permute-start(f32[16,32]{0,1:T(8,128)S(1)} %get-tuple-element.569), channel_id=1, source_target_pairs={{0,1},{1,2},{2,3},{3,4},{4,5},{5,6},{6,7},{7,0},{8,9},{9,10},{10,1... | collective-permute-start | bytes 6152 | tf_op jit(solution)/shard_map/while/body/eval_jaxpr/ppermute | solution.py:20
  129.6 10.9 %collective-permute-start.1 = (f32[16,4096]{1,0:T(8,128)S(1)}, f32[16,4096]{1,0:T(8,128)S(1)}, u32[]{:S(2)}, u32[]{:S(2)}) collective-permute-start(f32[16,4096]{1,0:T(8,128)S(1)} %fusion.72), channel_id=1, source_target_pairs={{0,1},{1,2},{2,3},{3,4},{4,5},{5,6},{6,7},{7,0},{8,9},{9,10},{10,1... | collective-permute-start | bytes 786440 | tf_op jit(solution)/shard_map/while/body/eval_jaxpr/ppermute | solution.py:20
  129.6 10.8 %collective-permute-start = (bf16[16,4096]{1,0:T(8,128)(2,1)S(1)}, bf16[16,4096]{1,0:T(8,128)(2,1)S(1)}, u32[]{:S(2)}, u32[]{:S(2)}) collective-permute-start(bf16[16,4096]{1,0:T(8,128)(2,1)S(1)} %copy.112), channel_id=1, source_target_pairs={{0,1},{1,2},{2,3},{3,4},{4,5},{5,6},{6,7},{7,0},{8,9},{9,10},{10,1... | collective-permute-start | bytes 393224 | tf_op jit(solution)/shard_map/while/body/eval_jaxpr/ppermute | solution.py:20
  129.8 10.7 %collective-permute-start.3 = (f32[16,32]{0,1:T(8,128)S(1)}, f32[16,32]{0,1:T(8,128)S(1)}, u32[]{:S(2)}, u32[]{:S(2)}) collective-permute-start(f32[16,32]{0,1:T(8,128)S(1)} %get-tuple-element.569), channel_id=1, source_target_pairs={{0,1},{1,2},{2,3},{3,4},{4,5},{5,6},{6,7},{7,0},{8,9},{9,10},{10,1... | collective-permute-start | bytes 6152 | tf_op jit(solution)/shard_map/while/body/eval_jaxpr/ppermute | solution.py:20
  (15 other events, 209.4 us)
